TPU v7x, 32 devices: a whole 2x2x4 slice. The times are simulated.
32 devices in a mesh: wide: 8 (over y, x, core), narrow: 4 (over z).
Axes of the slice: x: 2, y: 2, z: 4, core: 2. Of those that a mesh axis runs over, the one named last changes fastest.
Arguments:
- left: bfloat16 [32, 32, 256], P('narrow', None, 'wide'), may hold values from -6 to 6
- right: bfloat16 [32, 32, 256], P('wide', None, 'narrow'), may hold values from -6 to 6
- out_weight: bfloat16 [1024, 128], replicated, may hold values from -1 to 1
- out_bias: float32 [128], replicated, may hold values from -3 to 3
- cotangent: bfloat16 [256, 256, 128], P('wide', 'narrow'), may hold values from -0.5 to 0.5
Outputs:
- pair_update: bfloat16 [256, 256, 128], P('wide', 'narrow')
- grad_left: float32 [32, 32, 256], P('narrow', None, 'wide')
- grad_right: float32 [32, 32, 256], P('wide', None, 'narrow')
All inputs are finite; a program needn't handle non-finite values.
Results may differ from a plain program's by a relative error of at most 0.0045.
Values may be sent and summed in bfloat16 or wider, within the bound.
No kernel may reach another device: no remote copies, remote signals or barrier semaphores. Data moves between devices by JAX's collectives and lax.ppermute only.
A program may use at most 64 MiB of HBM per device.

v0:
```python
import math
import jax
import jax.numpy as jnp
from jax import lax
from jax.sharding import PartitionSpec as P


def local(left, right, out_weight, out_bias, cotangent):
    left_complete = lax.all_gather(left, "narrow", axis=0, tiled=True)
    right_full = lax.all_gather(right, "wide", axis=0, tiled=True)
    alignment_rows = left_complete.shape[0]
    channel_count = left_complete.shape[1]
    tile_rows = left_complete.shape[2]
    tile_columns = right_full.shape[2]
    pair_width = cotangent.shape[2]
    rows_per_block = math.gcd(16, tile_rows)
    total_block_count = tile_rows // rows_per_block
    kept_rows = alignment_rows // lax.axis_size("narrow")

    def block_step(block_index, carry):
        running, pairs, grads = carry
        start = (block_index * rows_per_block).astype(jnp.int32)
        left_block = lax.dynamic_slice_in_dim(left_complete, start, rows_per_block, 2)
        cot_block = lax.dynamic_slice_in_dim(cotangent, start, rows_per_block, 0)
        outer_sum = (
            jnp.einsum("sci,sej->ijce", left_block, right_full, preferred_element_type=jnp.float32)
            / alignment_rows
        )
        outer_flat = outer_sum.astype(jnp.bfloat16).reshape(
            rows_per_block * tile_columns, channel_count * channel_count
        )
        pair_out = jnp.dot(outer_flat, out_weight, preferred_element_type=jnp.float32) + out_bias
        pair_out = pair_out.astype(jnp.bfloat16).reshape(rows_per_block, tile_columns, pair_width)
        cot_flat = cot_block.reshape(rows_per_block * tile_columns, pair_width)
        d_outer = lax.dot_general(
            cot_flat, out_weight, (((1,), (1,)), ((), ())), preferred_element_type=jnp.float32
        )
        d_outer = d_outer.astype(jnp.bfloat16).reshape(
            rows_per_block, tile_columns, channel_count, channel_count
        )
        grad_block = (
            jnp.einsum("ijce,sej->sci", d_outer, right_full, preferred_element_type=jnp.float32)
            / alignment_rows
        )
        running = (
            running
            + jnp.einsum("ijce,sci->sej", d_outer, left_block, preferred_element_type=jnp.float32)
            / alignment_rows
        )
        grad_block = lax.psum_scatter(grad_block, "narrow", scatter_dimension=0, tiled=True)
        pairs = lax.dynamic_update_slice_in_dim(pairs, pair_out, start, 0)
        grads = lax.dynamic_update_slice_in_dim(grads, grad_block, start, 2)
        return (running, pairs, grads)

    starting_value = (
        jnp.zeros((alignment_rows, channel_count, tile_columns), jnp.float32),
        jnp.zeros((tile_rows, tile_columns, pair_width), jnp.bfloat16),
        jnp.zeros((kept_rows, channel_count, tile_rows), jnp.float32),
    )
    right_terms, pair_update, grad_terms = lax.fori_loop(
        0, total_block_count, block_step, starting_value
    )
    grad_right = lax.psum_scatter(right_terms, "wide", scatter_dimension=0, tiled=True)
    return (pair_update, grad_terms, grad_right)


def solution(mesh):
    return jax.shard_map(
        local,
        mesh=mesh,
        in_specs=(
            P("narrow", None, "wide"),
            P("wide", None, "narrow"),
            P(),
            P(),
            P("wide", "narrow", None),
        ),
        out_specs=(P("wide", "narrow", None), P("narrow", None, "wide"), P("wide", None, "narrow")),
        check_vma=False,
    )
```

profile of v0, /device:TPU:0, one launch (start us, length us, event | category | flops | bytes accessed | tf_op | source)
XLA Modules:
  0.0 147.1 jit_solution(11280594527067747907)
XLA Ops:
  8.0 0.9 copy.29
  9.0 14.5 %all_gather.6 = bf16[32,32,32]{1,0,2:T(8,128)(2,1)S(1)} all-gather(bf16[8,32,32]{1,0,2:T(8,128)(2,1)S(1)} %copy.29), channel_id=1, replica_groups=mesh['wide'=8,'narrow'=4] {'narrow'}, dimensions={0}, use_global_device_ids=true | all-gather | bytes 81920 | tf_op jit(solution)/shard_map/all_gather | solution.py:9
  23.4 9.5 %all_gather.7 = bf16[32,32,64]{2,1,0:T(8,128)(2,1)S(1)} all-gather(bf16[4,32,64]{2,1,0:T(8,128)(2,1)} %param.8), channel_id=1, replica_groups=mesh['wide'=8,'narrow'=4] {'wide'}, dimensions={0}, use_global_device_ids=true | all-gather | bytes 147456 | tf_op jit(solution)/shard_map/all_gather | solution.py:10
  33.0 0.1 copy.30
  33.1 0.1 broadcast_in_dim.13
  33.2 70.0 %while.18 = (s32[]{:T(128)}, f32[32,32,64]{2,0,1:T(8,128)}, bf16[32,64,128]{2,1,0:T(8,128)(2,1)S(1)}, f32[8,32,32]{1,2,0:T(8,128)S(1)}, bf16[32,32,32]{1,0,2:T(8...) while((s32[]{:T(128)}, f32[32,32,64]{2,0,1:T(8,128)}, ...), condition=%wide.region_2.0_spmd.clone, body=%wide.region_0.0_spmd.clone.sunk | while | flops 741818368 | bytes 32361256 | solution.py:60
  33.2 0.0 reduce-scatter.5.cloned.1.call-start
  33.3 1.0 constant_dynamic-slice_fusion.2
  34.2 3.0 %convolution_convert_fusion.2 = bf16[1024,1024]{1,0:T(8,128)(2,1)} fusion(bf16[1024,128]{1,0:T(8,128)(2,1)S(1)} %bitcast.82, bf16[1024,128]{1,0:T(8,128)(2,1)} %get-tuple-element.315), kind=kOutput, calls=%fused_computation.4.clone.1 | convolution fusion | flops 269484032 | bytes 2621440 | tf_op jit(solution)/shard_map/while/body/eval_jaxpr/dot_general | solution.py:35
  37.2 2.9 %copy.53 = bf16[1024,1024]{0,1:T(8,128)(2,1)S(1)} copy(bf16[1024,1024]{1,0:T(8,128)(2,1)} %convolution_convert_fusion.2) | data formatting | bytes 4194304 | tf_op jit(solution)/shard_map/while/body/eval_jaxpr/convert_element_type | solution.py:38
  40.1 4.0 %reshape.46 = bf16[16,64,32,32]{1,0,3,2:T(8,128)(2,1)} reshape(bf16[1024,1024]{0,1:T(8,128)(2,1)S(1)} %copy.53) | data formatting | bytes 4194304 | tf_op jit(solution)/shard_map/while/body/eval_jaxpr/reshape | solution.py:38
  44.1 3.4 %fusion.58 = f32[32,32,16]{0,2,1:T(8,128)S(1)} fusion(bf16[16,64,32,32]{1,0,3,2:T(8,128)(2,1)} %reshape.46, bf16[32,32,64]{2,0,1:T(8,128)(2,1)S(1)} %get-tuple-element.316), kind=kOutput, calls=%fused_computation.13.clone.1 | convolution fusion | flops 67125248 | bytes 2293760 | tf_op jit(solution)/shard_map/while/body/eval_jaxpr/ijce,sej->sci/dot_general | solution.py:42
  47.5 0.9 copy.55
  48.4 0.0 reduce-scatter.5.cloned.1.call-update
  48.4 1.3 fusion.56
  49.7 4.7 %copy.54 = bf16[16,64,32,32]{1,0,3,2:T(8,128)(2,1)} copy(bf16[16,64,32,32]{1,2,3,0:T(8,128)(2,1)S(1)} %fusion.56) | data formatting | bytes 4194304 | tf_op jit(solution)/shard_map/while/body/eval_jaxpr/convert_element_type | solution.py:29
  54.4 5.5 %reshape.47 = bf16[1024,1024]{0,1:T(8,128)(2,1)S(1)} reshape(bf16[16,64,32,32]{1,0,3,2:T(8,128)(2,1)} %copy.54) | data formatting | bytes 4194304 | tf_op jit(solution)/shard_map/while/body/eval_jaxpr/reshape | solution.py:29
  59.8 0.0 copy-start
  59.8 0.0 copy-start.2
  59.9 5.7 %fusion.55 = f32[32,32,64]{2,0,1:T(8,128)} fusion(bf16[16,64,32,32]{1,0,3,2:T(8,128)(2,1)} %reshape.46, f32[32,32,64]{2,0,1:T(8,128)} %get-tuple-element.297, pred[]{:T(512)S(6)} %compare.3, bf16[32,32,32]{1,0,2:T(8,128)(2,1)S(1)} %get-tuple-element.313, s32[]{:T(128)S(6)} %select_n.12), kind=kOutput, calls=%fused_computation.9.clone.1 | convolution fusion | flops 67305472 | bytes 2752517 | tf_op jit(solution)/shard_map/while/body/eval_jaxpr/ijce,sci->sej/dot_general | solution.py:47
  65.5 0.0 copy-done
  65.5 0.0 copy-done.2
  65.5 0.7 fusion.57
  66.3 1.6 %reduce-scatter.5.cloned.1.call-done = f32[8,32,16]{1,2,0:T(8,128)} async-done(((f32[32,32,16]{1,2,0:T(8,128)}), f32[8,32,16]{1,2,0:T(8,128)}) %reduce-scatter.5.cloned.1.call-update) | async-done | bytes 16400 | tf_op jit(solution)/shard_map/while/body/eval_jaxpr/reduce_scatter | solution.py:50
  67.9 0.8 constant_dynamic-update-slice_fusion.5
  68.8 0.0 reduce-scatter.5.cloned.1.call-start
  68.8 1.0 constant_dynamic-slice_fusion.2
  69.8 3.0 %convolution_convert_fusion.2 = bf16[1024,1024]{1,0:T(8,128)(2,1)} fusion(bf16[1024,128]{1,0:T(8,128)(2,1)S(1)} %bitcast.82, bf16[1024,128]{1,0:T(8,128)(2,1)} %get-tuple-element.315), kind=kOutput, calls=%fused_computation.4.clone.1 | convolution fusion | flops 269484032 | bytes 2621440 | tf_op jit(solution)/shard_map/while/body/eval_jaxpr/dot_general | solution.py:35
  72.8 2.9 %copy.53 = bf16[1024,1024]{0,1:T(8,128)(2,1)S(1)} copy(bf16[1024,1024]{1,0:T(8,128)(2,1)} %convolution_convert_fusion.2) | data formatting | bytes 4194304 | tf_op jit(solution)/shard_map/while/body/eval_jaxpr/convert_element_type | solution.py:38
  75.6 4.0 %reshape.46 = bf16[16,64,32,32]{1,0,3,2:T(8,128)(2,1)} reshape(bf16[1024,1024]{0,1:T(8,128)(2,1)S(1)} %copy.53) | data formatting | bytes 4194304 | tf_op jit(solution)/shard_map/while/body/eval_jaxpr/reshape | solution.py:38
  79.6 3.4 %fusion.58 = f32[32,32,16]{0,2,1:T(8,128)S(1)} fusion(bf16[16,64,32,32]{1,0,3,2:T(8,128)(2,1)} %reshape.46, bf16[32,32,64]{2,0,1:T(8,128)(2,1)S(1)} %get-tuple-element.316), kind=kOutput, calls=%fused_computation.13.clone.1 | convolution fusion | flops 67125248 | bytes 2293760 | tf_op jit(solution)/shard_map/while/body/eval_jaxpr/ijce,sej->sci/dot_general | solution.py:42
  83.0 0.9 copy.55
  83.9 0.0 reduce-scatter.5.cloned.1.call-update
  83.9 1.3 fusion.56
  85.2 4.7 %copy.54 = bf16[16,64,32,32]{1,0,3,2:T(8,128)(2,1)} copy(bf16[16,64,32,32]{1,2,3,0:T(8,128)(2,1)S(1)} %fusion.56) | data formatting | bytes 4194304 | tf_op jit(solution)/shard_map/while/body/eval_jaxpr/convert_element_type | solution.py:29
  89.9 5.5 %reshape.47 = bf16[1024,1024]{0,1:T(8,128)(2,1)S(1)} reshape(bf16[16,64,32,32]{1,0,3,2:T(8,128)(2,1)} %copy.54) | data formatting | bytes 4194304 | tf_op jit(solution)/shard_map/while/body/eval_jaxpr/reshape | solution.py:29
  95.4 0.0 copy-start
  95.4 0.0 copy-start.2
  95.4 5.8 %fusion.55 = f32[32,32,64]{2,0,1:T(8,128)} fusion(bf16[16,64,32,32]{1,0,3,2:T(8,128)(2,1)} %reshape.46, f32[32,32,64]{2,0,1:T(8,128)} %get-tuple-element.297, pred[]{:T(512)S(6)} %compare.3, bf16[32,32,32]{1,0,2:T(8,128)(2,1)S(1)} %get-tuple-element.313, s32[]{:T(128)S(6)} %select_n.12), kind=kOutput, calls=%fused_computation.9.clone.1 | convolution fusion | flops 67305472 | bytes 2752517 | tf_op jit(solution)/shard_map/while/body/eval_jaxpr/ijce,sci->sej/dot_general | solution.py:47
  101.2 0.0 copy-done
  101.2 0.0 copy-done.2
  101.2 0.7 fusion.57
  102.0 0.4 reduce-scatter.5.cloned.1.call-done
  102.4 0.8 constant_dynamic-update-slice_fusion.5
  103.2 0.0 copy-start.1
  103.2 0.0 reduce-scatter.3.cloned.1.call-start
  103.2 2.3 %copy.31 = f32[32,32,64]{2,1,0:T(8,128)} copy(f32[32,32,64]{2,0,1:T(8,128)} %get-tuple-element.161) | data formatting | bytes 524288 | tf_op jit(solution)/shard_map/while | solution.py:60
  105.6 0.0 reduce-scatter.3.cloned.1.call-update
  105.6 0.8 copy.32
  106.3 33.4 %reduce-scatter.3.cloned.1.call-done = f32[4,32,64]{2,1,0:T(8,128)} async-done(((f32[32,32,64]{2,1,0:T(8,128)}), f32[4,32,64]{2,1,0:T(8,128)}) %reduce-scatter.3.cloned.1.call-update) | async-done | bytes 32784 | tf_op jit(solution)/shard_map/reduce_scatter | solution.py:63
  139.7 0.0 copy-done.1
  (4 shorter events, 0.1 us)
Async XLA Ops:
  33.2 34.7 %reduce-scatter.5.cloned.1.call-start = ((), (), s32[]{:S(2)}) async-start(), calls=%async_computation.3 | async-start | bytes 327680 | tf_op jit(solution)/shard_map/while/body/eval_jaxpr/reduce_scatter | solution.py:50
  59.8 5.7 %copy-start = (bf16[1024,128]{1,0:T(8,128)(2,1)S(1)}, bf16[1024,128]{1,0:T(8,128)(2,1)}, u32[]{:S(2)}) copy-start(bf16[1024,128]{1,0:T(8,128)(2,1)} %get-tuple-element.315) | copy-start | bytes 786436 | tf_op jit(solution)/shard_map/while
  59.8 5.7 %copy-start.2 = (f32[128]{0:T(128)S(1)}, f32[128]{0:T(128)}, u32[]{:S(2)}) copy-start(f32[128]{0:T(128)} %get-tuple-element.317) | copy-start | bytes 1540 | tf_op jit(solution)/shard_map/while
  68.8 33.6 %reduce-scatter.5.cloned.1.call-start = ((), (), s32[]{:S(2)}) async-start(), calls=%async_computation.3 | async-start | bytes 327680 | tf_op jit(solution)/shard_map/while/body/eval_jaxpr/reduce_scatter | solution.py:50
  95.4 5.8 %copy-start = (bf16[1024,128]{1,0:T(8,128)(2,1)S(1)}, bf16[1024,128]{1,0:T(8,128)(2,1)}, u32[]{:S(2)}) copy-start(bf16[1024,128]{1,0:T(8,128)(2,1)} %get-tuple-element.315) | copy-start | bytes 786436 | tf_op jit(solution)/shard_map/while
  95.4 5.8 %copy-start.2 = (f32[128]{0:T(128)S(1)}, f32[128]{0:T(128)}, u32[]{:S(2)}) copy-start(f32[128]{0:T(128)} %get-tuple-element.317) | copy-start | bytes 1540 | tf_op jit(solution)/shard_map/while
  103.2 36.5 %copy-start.1 = (bf16[32,64,128]{2,1,0:T(8,128)(2,1)}, bf16[32,64,128]{2,1,0:T(8,128)(2,1)S(1)}, u32[]{:S(2)}) copy-start(bf16[32,64,128]{2,1,0:T(8,128)(2,1)S(1)} %get-tuple-element.207) | copy-start | bytes 1572868
  103.2 36.5 %reduce-scatter.3.cloned.1.call-start = ((), (), s32[]{:S(2)}) async-start(), calls=%async_computation.2 | async-start | bytes 589824 | tf_op jit(solution)/shard_map/reduce_scatter | solution.py:63
Sparse Core Ops, SparseCore 0:
  48.5 19.3 reduce-scatter.4
  84.0 18.2 reduce-scatter.4
Sparse Core Ops, SparseCore 1:
  107.3 32.3 reduce-scatter.2
where the time goes:
time: 148 us; the launch traced here: 147 us
  local copies, waits for them, and re-layouts  43.7 us (30%)
  waiting for transfers between devices  35.4 us (24%)
  matrix products  28.3 us (19%)
  blocking collectives  24 us (16%)
  between operations  15.5 us (10%)
    reduce_scatter x1, waiting for transfers between devices, local(): lax.psum_scatter(right_terms, 'wide', scatter_dimension=0, tiled=True)  33.4 us
    all_gather x1, blocking collectives, local(): left_complete = lax.all_gather(left, 'narrow', axis=0, tiled=True)  14.5 us
    dot_general x2, matrix products, block_step(): jnp.einsum('ijce,sci->sej', d_outer, left_block, preferred_element_type=j...  11.5 us
    reshape x2, local copies, waits for them, and re-layouts, block_step(): outer_sum.astype(jnp.bfloat16)  10.9 us
    all_gather x1, blocking collectives, local(): right_full = lax.all_gather(right, 'wide', axis=0, tiled=True)  9.51 us
    convert_element_type x2, local copies, waits for them, and re-layouts, block_step(): outer_sum.astype(jnp.bfloat16)  9.33 us
    reshape x2, local copies, waits for them, and re-layouts, block_step(): d_outer.astype(jnp.bfloat16)  7.98 us
    dot_general x2, matrix products, block_step(): jnp.einsum('ijce,sej->sci', d_outer, right_full, preferred_element_type=j...  6.81 us
  transfers between devices with their start and end apart: 3, of which 3 were waited for; matrix products, arithmetic and copies ran while one was open for 25% of the time, Pallas kernels for 0%

commit v1 on v0

--- a/solution.py
+++ b/solution.py
@@ -6,7 +6,14 @@
 
 
 def local(left, right, out_weight, out_bias, cotangent):
-    left_complete = lax.all_gather(left, "narrow", axis=0, tiled=True)
+    ring = [left]
+    for hop in range(3):
+        ring.append(lax.ppermute(ring[-1], "narrow", [(dev, (dev + 1) % 4) for dev in range(4)]))
+    left_complete = jnp.roll(
+        jnp.concatenate(ring[::-1], axis=0),
+        (lax.axis_index("narrow") + 1) * ring[0].shape[0],
+        axis=0,
+    )
     right_full = lax.all_gather(right, "wide", axis=0, tiled=True)
     alignment_rows = left_complete.shape[0]
     channel_count = left_complete.shape[1]

time: 148 us -> 149 us (level)
  blocking collectives: 24 us -> 9.73 us
  waiting for transfers between devices: 35.4 us -> 46.8 us
  starting transfers between devices: 0.08 us -> 3.19 us
    all_gather x1 -> x0, blocking collectives: 14.5 us -> none  [local(): left_complete = lax.all_gather(left, 'narrow', axis=0, tiled=True)]
    ppermute x0 -> x3, waiting for transfers between devices: none -> 10.3 us  [local(): lax.ppermute(ring[-1], 'narrow', [(dev, (dev + 1) % 4) for dev in range(4)])]
    ppermute x0 -> x3, starting transfers between devices: none -> 3.11 us  [local(): lax.ppermute(ring[-1], 'narrow', [(dev, (dev + 1) % 4) for dev in range(4)])]
  transfers between devices with their start and end apart: 3 -> 6, of which waited for: 3 -> 5; matrix products, arithmetic and copies ran while one was open for 25% -> 25% of each run, Pallas kernels for 0% -> 0%
where the time goes in v1:
time: 149 us; the launch traced here: 148 us
  waiting for transfers between devices  46.8 us (31%)
  local copies, waits for them, and re-layouts  44 us (30%)
  matrix products  28.3 us (19%)
  between operations  15.6 us (10%)
  blocking collectives  9.73 us (7%)
  starting transfers between devices  3.19 us (2%)
    reduce_scatter x1, waiting for transfers between devices, local(): lax.psum_scatter(right_terms, 'wide', scatter_dimension=0, tiled=True)  33.4 us
    dot_general x2, matrix products, block_step(): jnp.einsum('ijce,sci->sej', d_outer, left_block, preferred_element_type=j...  11.5 us
    reshape x2, local copies, waits for them, and re-layouts, block_step(): outer_sum.astype(jnp.bfloat16)  11 us
    ppermute x3, waiting for transfers between devices, local(): lax.ppermute(ring[-1], 'narrow', [(dev, (dev + 1) % 4) for dev in range(4)])  10.3 us
    all_gather x1, blocking collectives, local(): right_full = lax.all_gather(right, 'wide', axis=0, tiled=True)  9.73 us
    convert_element_type x2, local copies, waits for them, and re-layouts, block_step(): outer_sum.astype(jnp.bfloat16)  9.37 us
    reshape x2, local copies, waits for them, and re-layouts, block_step(): d_outer.astype(jnp.bfloat16)  8.03 us
    dot_general x2, matrix products, block_step(): jnp.einsum('ijce,sej->sci', d_outer, right_full, preferred_element_type=j...  6.81 us
  transfers between devices with their start and end apart: 6, of which 5 were waited for; matrix products, arithmetic and copies ran while one was open for 25% of the time, Pallas kernels for 0%

profile of v1, /device:TPU:0, one launch (start us, length us, event | category | flops | bytes accessed | tf_op | source)
XLA Modules:
  0.0 147.7 jit_solution(10675459022013286093)
XLA Ops:
  8.0 0.9 copy.33
  8.9 3.1 %collective-permute-start = (bf16[8,32,32]{1,0,2:T(8,128)(2,1)S(1)}, bf16[8,32,32]{1,0,2:T(8,128)(2,1)S(1)}, u32[]{:S(2)}, u32[]{:S(2)}) collective-permute-start(bf16[8,32,32]{1,0,2:T(8,128)(2,1)S(1)} %copy.33), channel_id=1, source_target_pairs={{0,1},{1,2},{2,3},{3,0},{4,5},{5,6},{6,7},{7,4},{8,9},{9,10},{10,1... | collective-permute-start | bytes 49160 | tf_op jit(solution)/shard_map/ppermute | solution.py:11
  12.0 4.3 %collective-permute-done = bf16[8,32,32]{1,0,2:T(8,128)(2,1)S(1)} collective-permute-done((bf16[8,32,32]{1,0,2:T(8,128)(2,1)S(1)}, bf16[8,32,32]{1,0,2:T(8,128)(2,1)S(1)}, u32[]{:S(2)}, u32[]{:S(2)}) %collective-permute-start) | collective-permute-done | bytes 16416 | tf_op jit(solution)/shard_map/ppermute | solution.py:11
  16.3 0.0 collective-permute-start.1
  16.3 6.1 %collective-permute-done.1 = bf16[8,32,32]{1,0,2:T(8,128)(2,1)S(1)} collective-permute-done((bf16[8,32,32]{1,0,2:T(8,128)(2,1)S(1)}, bf16[8,32,32]{1,0,2:T(8,128)(2,1)S(1)}, u32[]{:S(2)}, u32[]{:S(2)}) %collective-permute-start.1) | collective-permute-done | bytes 16416 | tf_op jit(solution)/shard_map/ppermute | solution.py:11
  22.4 0.0 collective-permute-start.2
  22.4 9.7 %all_gather.3 = bf16[32,32,64]{2,1,0:T(8,128)(2,1)S(1)} all-gather(bf16[4,32,64]{2,1,0:T(8,128)(2,1)} %param.8), channel_id=1, replica_groups=mesh['wide'=8,'narrow'=4] {'wide'}, dimensions={0}, use_global_device_ids=true | all-gather | bytes 147456 | tf_op jit(solution)/shard_map/all_gather | solution.py:17
  32.1 0.1 copy.36
  32.2 0.0 collective-permute-done.2
  32.5 0.1 broadcast_in_dim.13
  32.6 71.2 %while.18 = (s32[]{:T(128)}, f32[32,32,64]{2,0,1:T(8,128)}, bf16[32,64,128]{2,1,0:T(8,128)(2,1)S(1)}, f32[8,32,32]{1,2,0:T(8,128)S(1)}, bf16[32,32,32]{1,0,2:T(8...) while((s32[]{:T(128)}, f32[32,32,64]{2,0,1:T(8,128)}, ...), condition=%wide.region_2.3_spmd.clone, body=%wide.region_0.2_spmd.clone.sunk | while | flops 741818368 | bytes 32361256 | solution.py:67
  32.6 0.0 reduce-scatter.5.cloned.1.call-start
  32.7 1.0 constant_dynamic-slice_fusion.3
  33.7 3.0 %convolution_convert_fusion.2 = bf16[1024,1024]{1,0:T(8,128)(2,1)} fusion(bf16[1024,128]{1,0:T(8,128)(2,1)S(1)} %bitcast.82, bf16[1024,128]{1,0:T(8,128)(2,1)} %get-tuple-element.315), kind=kOutput, calls=%fused_computation.4.clone.1 | convolution fusion | flops 269484032 | bytes 2621440 | tf_op jit(solution)/shard_map/while/body/eval_jaxpr/dot_general | solution.py:42
  36.7 2.9 %copy.59 = bf16[1024,1024]{0,1:T(8,128)(2,1)S(1)} copy(bf16[1024,1024]{1,0:T(8,128)(2,1)} %convolution_convert_fusion.2) | data formatting | bytes 4194304 | tf_op jit(solution)/shard_map/while/body/eval_jaxpr/convert_element_type | solution.py:45
  39.5 4.0 %reshape.46 = bf16[16,64,32,32]{1,0,3,2:T(8,128)(2,1)} reshape(bf16[1024,1024]{0,1:T(8,128)(2,1)S(1)} %copy.59) | data formatting | bytes 4194304 | tf_op jit(solution)/shard_map/while/body/eval_jaxpr/reshape | solution.py:45
  43.5 3.4 %fusion.58 = f32[32,32,16]{0,2,1:T(8,128)S(1)} fusion(bf16[16,64,32,32]{1,0,3,2:T(8,128)(2,1)} %reshape.46, bf16[32,32,64]{2,0,1:T(8,128)(2,1)S(1)} %get-tuple-element.316), kind=kOutput, calls=%fused_computation.13.clone.1 | convolution fusion | flops 67125248 | bytes 2293760 | tf_op jit(solution)/shard_map/while/body/eval_jaxpr/ijce,sej->sci/dot_general | solution.py:49
  47.0 0.9 copy.61
  47.8 0.0 reduce-scatter.5.cloned.1.call-update
  47.9 1.3 fusion.56
  49.1 4.7 %copy.60 = bf16[16,64,32,32]{1,0,3,2:T(8,128)(2,1)} copy(bf16[16,64,32,32]{1,2,3,0:T(8,128)(2,1)S(1)} %fusion.56) | data formatting | bytes 4194304 | tf_op jit(solution)/shard_map/while/body/eval_jaxpr/convert_element_type | solution.py:36
  53.8 5.5 %reshape.47 = bf16[1024,1024]{0,1:T(8,128)(2,1)S(1)} reshape(bf16[16,64,32,32]{1,0,3,2:T(8,128)(2,1)} %copy.60) | data formatting | bytes 4194304 | tf_op jit(solution)/shard_map/while/body/eval_jaxpr/reshape | solution.py:36
  59.3 0.0 copy-start
  59.3 0.0 copy-start.2
  59.3 5.7 %fusion.55 = f32[32,32,64]{2,0,1:T(8,128)} fusion(bf16[16,64,32,32]{1,0,3,2:T(8,128)(2,1)} %reshape.46, f32[32,32,64]{2,0,1:T(8,128)} %get-tuple-element.297, pred[]{:T(512)S(6)} %compare.4, bf16[32,32,32]{1,0,2:T(8,128)(2,1)S(1)} %get-tuple-element.313, s32[]{:T(128)S(6)} %select_n.27), kind=kOutput, calls=%fused_computation.9.clone.1 | convolution fusion | flops 67305472 | bytes 2752517 | tf_op jit(solution)/shard_map/while/body/eval_jaxpr/ijce,sci->sej/dot_general | solution.py:54
  65.0 0.0 copy-done
  65.0 0.0 copy-done.2
  65.0 0.7 fusion.57
  65.8 2.7 %reduce-scatter.5.cloned.1.call-done = f32[8,32,16]{1,2,0:T(8,128)} async-done(((f32[32,32,16]{1,2,0:T(8,128)}), f32[8,32,16]{1,2,0:T(8,128)}) %reduce-scatter.5.cloned.1.call-update) | async-done | bytes 16400 | tf_op jit(solution)/shard_map/while/body/eval_jaxpr/reduce_scatter | solution.py:57
  68.5 0.8 constant_dynamic-update-slice_fusion.13
  69.3 0.0 reduce-scatter.5.cloned.1.call-start
  69.3 1.0 constant_dynamic-slice_fusion.3
  70.3 3.0 %convolution_convert_fusion.2 = bf16[1024,1024]{1,0:T(8,128)(2,1)} fusion(bf16[1024,128]{1,0:T(8,128)(2,1)S(1)} %bitcast.82, bf16[1024,128]{1,0:T(8,128)(2,1)} %get-tuple-element.315), kind=kOutput, calls=%fused_computation.4.clone.1 | convolution fusion | flops 269484032 | bytes 2621440 | tf_op jit(solution)/shard_map/while/body/eval_jaxpr/dot_general | solution.py:42
  73.3 2.9 %copy.59 = bf16[1024,1024]{0,1:T(8,128)(2,1)S(1)} copy(bf16[1024,1024]{1,0:T(8,128)(2,1)} %convolution_convert_fusion.2) | data formatting | bytes 4194304 | tf_op jit(solution)/shard_map/while/body/eval_jaxpr/convert_element_type | solution.py:45
  76.2 4.0 %reshape.46 = bf16[16,64,32,32]{1,0,3,2:T(8,128)(2,1)} reshape(bf16[1024,1024]{0,1:T(8,128)(2,1)S(1)} %copy.59) | data formatting | bytes 4194304 | tf_op jit(solution)/shard_map/while/body/eval_jaxpr/reshape | solution.py:45
  80.2 3.4 %fusion.58 = f32[32,32,16]{0,2,1:T(8,128)S(1)} fusion(bf16[16,64,32,32]{1,0,3,2:T(8,128)(2,1)} %reshape.46, bf16[32,32,64]{2,0,1:T(8,128)(2,1)S(1)} %get-tuple-element.316), kind=kOutput, calls=%fused_computation.13.clone.1 | convolution fusion | flops 67125248 | bytes 2293760 | tf_op jit(solution)/shard_map/while/body/eval_jaxpr/ijce,sej->sci/dot_general | solution.py:49
  83.6 0.9 copy.61
  84.5 0.0 reduce-scatter.5.cloned.1.call-update
  84.5 1.3 fusion.56
  85.8 4.7 %copy.60 = bf16[16,64,32,32]{1,0,3,2:T(8,128)(2,1)} copy(bf16[16,64,32,32]{1,2,3,0:T(8,128)(2,1)S(1)} %fusion.56) | data formatting | bytes 4194304 | tf_op jit(solution)/shard_map/while/body/eval_jaxpr/convert_element_type | solution.py:36
  90.5 5.5 %reshape.47 = bf16[1024,1024]{0,1:T(8,128)(2,1)S(1)} reshape(bf16[16,64,32,32]{1,0,3,2:T(8,128)(2,1)} %copy.60) | data formatting | bytes 4194304 | tf_op jit(solution)/shard_map/while/body/eval_jaxpr/reshape | solution.py:36
  96.0 0.0 copy-start
  96.0 0.0 copy-start.2
  96.0 5.8 %fusion.55 = f32[32,32,64]{2,0,1:T(8,128)} fusion(bf16[16,64,32,32]{1,0,3,2:T(8,128)(2,1)} %reshape.46, f32[32,32,64]{2,0,1:T(8,128)} %get-tuple-element.297, pred[]{:T(512)S(6)} %compare.4, bf16[32,32,32]{1,0,2:T(8,128)(2,1)S(1)} %get-tuple-element.313, s32[]{:T(128)S(6)} %select_n.27), kind=kOutput, calls=%fused_computation.9.clone.1 | convolution fusion | flops 67305472 | bytes 2752517 | tf_op jit(solution)/shard_map/while/body/eval_jaxpr/ijce,sci->sej/dot_general | solution.py:54
  101.8 0.0 copy-done
  101.8 0.0 copy-done.2
  101.8 0.7 fusion.57
  102.6 0.3 reduce-scatter.5.cloned.1.call-done
  102.9 0.8 constant_dynamic-update-slice_fusion.13
  103.8 0.0 copy-start.1
  103.8 0.0 reduce-scatter.3.cloned.1.call-start
  103.8 2.3 %copy.37 = f32[32,32,64]{2,1,0:T(8,128)} copy(f32[32,32,64]{2,0,1:T(8,128)} %get-tuple-element.161) | data formatting | bytes 524288 | tf_op jit(solution)/shard_map/while | solution.py:67
  106.1 0.0 reduce-scatter.3.cloned.1.call-update
  106.1 0.8 copy.38
  106.9 33.4 %reduce-scatter.3.cloned.1.call-done = f32[4,32,64]{2,1,0:T(8,128)} async-done(((f32[32,32,64]{2,1,0:T(8,128)}), f32[4,32,64]{2,1,0:T(8,128)}) %reduce-scatter.3.cloned.1.call-update) | async-done | bytes 32784 | tf_op jit(solution)/shard_map/reduce_scatter | solution.py:70
  140.3 0.0 copy-done.1
  (13 shorter events, 0.3 us)
Async XLA Ops:
  8.9 7.4 %collective-permute-start = (bf16[8,32,32]{1,0,2:T(8,128)(2,1)S(1)}, bf16[8,32,32]{1,0,2:T(8,128)(2,1)S(1)}, u32[]{:S(2)}, u32[]{:S(2)}) collective-permute-start(bf16[8,32,32]{1,0,2:T(8,128)(2,1)S(1)} %copy.33), channel_id=1, source_target_pairs={{0,1},{1,2},{2,3},{3,0},{4,5},{5,6},{6,7},{7,4},{8,9},{9,10},{10,1... | collective-permute-start | bytes 49160 | tf_op jit(solution)/shard_map/ppermute | solution.py:11
  16.3 6.1 %collective-permute-start.1 = (bf16[8,32,32]{1,0,2:T(8,128)(2,1)S(1)}, bf16[8,32,32]{1,0,2:T(8,128)(2,1)S(1)}, u32[]{:S(2)}, u32[]{:S(2)}) collective-permute-start(bf16[8,32,32]{1,0,2:T(8,128)(2,1)S(1)} %collective-permute-done), channel_id=1, source_target_pairs={{0,1},{1,2},{2,3},{3,0},{4,5},{5,6},{6,7},{7,4},{8,9},{9,10},{10,1... | collective-permute-start | bytes 49160 | tf_op jit(solution)/shard_map/ppermute | solution.py:11
  22.4 9.8 %collective-permute-start.2 = (bf16[8,32,32]{1,0,2:T(8,128)(2,1)S(1)}, bf16[8,32,32]{1,0,2:T(8,128)(2,1)S(1)}, u32[]{:S(2)}, u32[]{:S(2)}) collective-permute-start(bf16[8,32,32]{1,0,2:T(8,128)(2,1)S(1)} %collective-permute-done.1), channel_id=1, source_target_pairs={{0,1},{1,2},{2,3},{3,0},{4,5},{5,6},{6,7},{7,4},{8,9},{9,10},{10,1... | collective-permute-start | bytes 49160 | tf_op jit(solution)/shard_map/ppermute | solution.py:11
  32.6 35.9 %reduce-scatter.5.cloned.1.call-start = ((), (), s32[]{:S(2)}) async-start(), calls=%async_computation.3 | async-start | bytes 327680 | tf_op jit(solution)/shard_map/while/body/eval_jaxpr/reduce_scatter | solution.py:57
  59.3 5.7 %copy-start = (bf16[1024,128]{1,0:T(8,128)(2,1)S(1)}, bf16[1024,128]{1,0:T(8,128)(2,1)}, u32[]{:S(2)}) copy-start(bf16[1024,128]{1,0:T(8,128)(2,1)} %get-tuple-element.315) | copy-start | bytes 786436 | tf_op jit(solution)/shard_map/while
  59.3 5.7 %copy-start.2 = (f32[128]{0:T(128)S(1)}, f32[128]{0:T(128)}, u32[]{:S(2)}) copy-start(f32[128]{0:T(128)} %get-tuple-element.317) | copy-start | bytes 1540 | tf_op jit(solution)/shard_map/while
  69.3 33.6 %reduce-scatter.5.cloned.1.call-start = ((), (), s32[]{:S(2)}) async-start(), calls=%async_computation.3 | async-start | bytes 327680 | tf_op jit(solution)/shard_map/while/body/eval_jaxpr/reduce_scatter | solution.py:57
  96.0 5.8 %copy-start = (bf16[1024,128]{1,0:T(8,128)(2,1)S(1)}, bf16[1024,128]{1,0:T(8,128)(2,1)}, u32[]{:S(2)}) copy-start(bf16[1024,128]{1,0:T(8,128)(2,1)} %get-tuple-element.315) | copy-start | bytes 786436 | tf_op jit(solution)/shard_map/while
  96.0 5.8 %copy-start.2 = (f32[128]{0:T(128)S(1)}, f32[128]{0:T(128)}, u32[]{:S(2)}) copy-start(f32[128]{0:T(128)} %get-tuple-element.317) | copy-start | bytes 1540 | tf_op jit(solution)/shard_map/while
  103.8 36.5 %copy-start.1 = (bf16[32,64,128]{2,1,0:T(8,128)(2,1)}, bf16[32,64,128]{2,1,0:T(8,128)(2,1)S(1)}, u32[]{:S(2)}) copy-start(bf16[32,64,128]{2,1,0:T(8,128)(2,1)S(1)} %get-tuple-element.207) | copy-start | bytes 1572868
  103.8 36.5 %reduce-scatter.3.cloned.1.call-start = ((), (), s32[]{:S(2)}) async-start(), calls=%async_computation.2 | async-start | bytes 589824 | tf_op jit(solution)/shard_map/reduce_scatter | solution.py:70
Sparse Core Ops, SparseCore 0:
  48.0 20.4 reduce-scatter.4
  84.6 18.2 reduce-scatter.4
Sparse Core Ops, SparseCore 1:
  107.9 32.3 reduce-scatter.2
